TPU v7x, 32 devices: a whole 2x2x4 slice. The times are simulated.
32 devices in a mesh: pts: 8 (over y, x, core), cand: 4 (over z).
Axes of the slice: x: 2, y: 2, z: 4, core: 2. Of those that a mesh axis runs over, the one named last changes fastest.
Arguments:
- points: bfloat16 [8192, 1024], P('pts'), may hold values from -6 to 6
- weights: float32 [8192], P('pts'), may hold values from 0.5 to 5
- coverage: float32 [8192], P('pts'), may hold values from -0.5 to 1
- candidates: bfloat16 [4096, 1024], P('cand'), may hold values from -6 to 6
- picks: int32 [64], replicated, may hold values from 0 to 4095
Outputs:
- gains: float32 [4096], P('cand')
- top_gains: float32 [64], replicated
- new_coverage: float32 [8192], P('pts')
All inputs are finite; a program needn't handle non-finite values.
Results may differ from a plain program's by a relative error of at most 0.0003.
Values may be sent and summed in bfloat16 or wider, within the bound.
A program may use at most 64 MiB of HBM per device.

v0:
```python
import jax
import jax.numpy as jnp
from jax import lax
from jax.sharding import PartitionSpec as P

TOPK = 64


def joined(x, axis, combine):
    everything = lax.all_gather(x, axis)
    leading = everything[0]

    def hop(k, so_far):
        return combine(so_far, everything[k])

    return lax.fori_loop(1, lax.axis_size(axis), hop, leading)


def best_values(first, second):
    return lax.top_k(jnp.concatenate([first, second]), TOPK)[0]


def on_device(points, weights, coverage, candidates, picks):
    scale = points.shape[1] ** (-0.5)
    total = points.shape[0] * lax.axis_size("pts")
    cand_rows = candidates.shape[0]
    offset = lax.axis_index("cand") * cand_rows
    sims = jnp.dot(points, candidates.T, preferred_element_type=jnp.float32) * scale
    partial_value = (
        jnp.sum(weights[:, None] * jnp.maximum(sims - coverage[:, None], 0.0), axis=0) / total
    )
    gains = lax.psum(partial_value, "pts")
    top_gains = joined(lax.top_k(gains, TOPK)[0], "cand", best_values)
    columns = offset + jnp.arange(cand_rows, dtype=jnp.int32)
    chosen = jnp.any(picks[:, None] == columns[None, :], axis=0)
    local_best = jnp.max(jnp.where(chosen[None, :], sims, -1e30), axis=1)
    best_sim = lax.pmax(local_best, "cand")
    new_coverage = jnp.maximum(coverage, best_sim)
    return (gains, top_gains, new_coverage)


def solution(mesh):
    placed = (P("pts", None), P("pts"), P("pts"), P("cand", None), P())
    return jax.shard_map(
        on_device, mesh=mesh, in_specs=placed, out_specs=(P("cand"), P(), P("pts")), check_vma=False
    )
```

profile of v0, /device:TPU:0, one launch (start us, length us, event | category | flops | bytes accessed | tf_op | source)
XLA Modules:
  0.0 56.5 jit_solution(17969848759909569890)
XLA Ops:
  0.6 0.0 copy-start
  0.7 0.9 %compare_reduce_fusion = pred[1024]{0:T(1024)(128)(4,1)S(1)} fusion(s32[1024]{0:T(1024)S(1)} %iota_add_fusion, s32[64]{0:T(128)} %param.11), kind=kLoop, calls=%fused_computation.4 | loop fusion | flops 130048 | bytes 5376 | tf_op jit(solution)/shard_map/reduce_or | solution.py:35
  1.6 0.7 %copy-done = bf16[1024,1024]{1,0:T(8,128)(2,1)S(1)} copy-done((bf16[1024,1024]{1,0:T(8,128)(2,1)S(1)}, bf16[1024,1024]{1,0:T(8,128)(2,1)}, u32[]{:S(2)}) %copy-start) | copy-done | bytes 2097176
  2.2 0.0 copy-start.3
  2.2 0.0 copy-start.2
  2.2 4.4 %select_reduce_fusion = (f32[1024]{0:T(1024)S(1)}, f32[1024]{0:T(1024)S(1)}) fusion(pred[1024]{0:T(1024)(128)(4,1)S(1)} %compare_reduce_fusion, f32[1024]{0:T(1024)} %param.9, f32[1024]{0:T(1024)} %param.8, bf16[1024,1024]{1,0:T(8,128)(2,1)S(1)} %copy-done, bf16[1024,1024]{1,0:T(8,128)(2,1)} %param.10), kind=kOutput, calls=%fused_computation.2 | convolution fusion | flops 2154821632 | bytes 4211712 | tf_op jit(solution)/shard_map/dot_general | solution.py:28
  6.6 15.2 %psum.7 = f32[1024]{0:T(1024)S(1)} all-reduce(f32[1024]{0:T(1024)S(1)} %broadcast_multiply_fusion), channel_id=1, replica_groups=mesh['pts'=8,'cand'=4] {'pts'}, use_global_device_ids=true, to_apply=%region_1.0 | all-reduce | flops 1024 | bytes 8192 | tf_op jit(solution)/shard_map/psum | solution.py:32
  21.8 0.0 copy-start.1
  21.8 4.4 %top_k.14 = (f32[1024]{0:T(1024)S(1)}, s32[1024]{0:T(1024)}) sort(f32[1024]{0:T(1024)S(1)} %psum.7, s32[1024]{0:T(1024)S(1)} %iota.11), dimensions={0}, to_apply=%region_2.0 | sort | flops 10240 | bytes 16384 | tf_op jit(solution)/shard_map/top_k | solution.py:33
  26.2 0.0 copy-done.3
  26.2 0.6 %dynamic-slice = u32[1]{0:T(128)} dynamic-slice(u32[32]{0:T(128)S(1)} %copy-done.3, u32[]{:T(128)S(6)} %add.47), dynamic_slice_sizes={1} | dynamic-slice | bytes 12
  27.5 0.1 slice_dynamic-update-slice_fusion
  27.6 11.9 %all-reduce = f32[256]{0:T(256)S(1)} all-reduce(f32[256]{0:T(256)S(1)} %slice_dynamic-update-slice_fusion), channel_id=2, replica_groups=mesh['pts'=8,'cand'=4] {'cand'}, use_global_device_ids=true, to_apply=%add | all-reduce | flops 256 | bytes 2048
  39.5 0.1 reshape.14
  39.6 8.0 %while.15 = (s32[]{:T(128)}, f32[64]{0:T(128)S(1)}, f32[4,64]{1,0:T(4,128)S(1)}, s32[]{:T(128)}, s32[]{:T(128)}, /*index=5*/s32[]{:T(128)}) while((s32[]{:T(128)}, f32[64]{0:T(128)S(1)}, f32[4,64]{1,0:T(4,128)S(1)}, s32[]{:T(128)}, s32[]{:T(128)}, /*index=5*/s32[]{:T(128)}) %tuple.41), condition=%wide.region_5.6_spmd, body=%wide.region_3.5_spmd.sunk | while | flops 1029 | bytes 4211 | solution.py:16
  39.6 0.1 pad_maximum_fusion.2
  39.7 2.6 %top_k.22 = (f32[128]{0:T(128)S(1)}, s32[128]{0:T(128)}) sort(f32[128]{0:T(128)S(1)} %pad_maximum_fusion.2, s32[128]{0:T(128)S(1)} %iota.15), dimensions={0}, to_apply=%region_4.4 | sort | flops 896 | bytes 2048 | tf_op jit(solution)/shard_map/while/body/eval_jaxpr/top_k | solution.py:20
  42.2 0.1 pad_maximum_fusion.2
  42.3 2.6 %top_k.22 = (f32[128]{0:T(128)S(1)}, s32[128]{0:T(128)}) sort(f32[128]{0:T(128)S(1)} %pad_maximum_fusion.2, s32[128]{0:T(128)S(1)} %iota.15), dimensions={0}, to_apply=%region_4.4 | sort | flops 896 | bytes 2048 | tf_op jit(solution)/shard_map/while/body/eval_jaxpr/top_k | solution.py:20
  44.9 0.1 pad_maximum_fusion.2
  45.0 2.6 %top_k.22 = (f32[128]{0:T(128)S(1)}, s32[128]{0:T(128)}) sort(f32[128]{0:T(128)S(1)} %pad_maximum_fusion.2, s32[128]{0:T(128)S(1)} %iota.15), dimensions={0}, to_apply=%region_4.4 | sort | flops 896 | bytes 2048 | tf_op jit(solution)/shard_map/while/body/eval_jaxpr/top_k | solution.py:20
  47.5 0.0 copy-start.4
  47.5 8.3 %pmax.7 = f32[1024]{0:T(1024)S(1)} all-reduce(f32[1024]{0:T(1024)S(1)} %get-tuple-element.97), channel_id=1, replica_groups=mesh['pts'=8,'cand'=4] {'cand'}, use_global_device_ids=true, to_apply=%region_8.9 | all-reduce | flops 1024 | bytes 8192 | tf_op jit(solution)/shard_map/pmax | solution.py:37
  55.9 0.0 copy-done.2
  55.9 0.6 %max.13 = f32[1024]{0:T(1024)} maximum(f32[1024]{0:T(1024)S(1)} %copy-done.2, f32[1024]{0:T(1024)S(1)} %pmax.7) | non-fusion elementwise | flops 1024 | bytes 12288 | tf_op jit(solution)/shard_map/max | solution.py:38
  56.5 0.0 copy-done.1
  56.5 0.0 copy-done.4
  (11 shorter events, 0.0 us)
Async XLA Ops:
  0.6 1.6 %copy-start = (bf16[1024,1024]{1,0:T(8,128)(2,1)S(1)}, bf16[1024,1024]{1,0:T(8,128)(2,1)}, u32[]{:S(2)}) copy-start(bf16[1024,1024]{1,0:T(8,128)(2,1)} %param.7) | copy-start | bytes 6291460
  2.2 24.0 %copy-start.3 = (u32[32]{0:T(128)S(1)}, u32[32]{0:T(128)}, u32[]{:S(2)}) copy-start(u32[32]{0:T(128)} %constant.74) | copy-start | bytes 388
  2.2 53.6 %copy-start.2 = (f32[1024]{0:T(1024)S(1)}, f32[1024]{0:T(1024)}, u32[]{:S(2)}) copy-start(f32[1024]{0:T(1024)} %param.9) | copy-start | bytes 12292
  21.8 34.7 %copy-start.1 = (f32[1024]{0:T(1024)}, f32[1024]{0:T(1024)S(1)}, u32[]{:S(2)}) copy-start(f32[1024]{0:T(1024)S(1)} %psum.7) | copy-start | bytes 12292
  47.5 8.9 %copy-start.4 = (f32[64]{0:T(128)}, f32[64]{0:T(128)S(1)}, u32[]{:S(2)}) copy-start(f32[64]{0:T(128)S(1)} %get-tuple-element.93) | copy-start | bytes 772
where the time goes:
time: 56.7 us; the launch traced here: 56.5 us
  blocking collectives  35.4 us (62%)
  other arithmetic  13.9 us (25%)
  matrix products  4.37 us (8%)
  local copies, waits for them, and re-layouts  1.48 us (3%)
  between operations  1.34 us (2%)
    psum x1, blocking collectives, on_device(): gains = lax.psum(partial_value, 'pts')  15.2 us
    unnamed x1, blocking collectives  11.9 us
    pmax x1, blocking collectives, on_device(): best_sim = lax.pmax(local_best, 'cand')  8.34 us
    top_k x3, other arithmetic, best_values(): return lax.top_k(jnp.concatenate([first, second]), TOPK)[0]  7.7 us
    top_k x1, other arithmetic, on_device(): top_gains = joined(lax.top_k(gains, TOPK)[0], 'cand', best_values)  4.43 us
    dot_general x1, matrix products, on_device(): jnp.dot(points, candidates.T, preferred_element_type=jnp.float32) * scale  4.37 us
    unnamed x13, local copies, waits for them, and re-layouts  1.37 us

commit v1 on v0

--- a/solution.py
+++ b/solution.py
@@ -29,7 +29,8 @@
     partial_value = (
         jnp.sum(weights[:, None] * jnp.maximum(sims - coverage[:, None], 0.0), axis=0) / total
     )
-    gains = lax.psum(partial_value, "pts")
+    y1 = lax.all_gather(partial_value, "pts")
+    gains = jnp.sum(y1, axis=0)
     top_gains = joined(lax.top_k(gains, TOPK)[0], "cand", best_values)
     columns = offset + jnp.arange(cand_rows, dtype=jnp.int32)
     chosen = jnp.any(picks[:, None] == columns[None, :], axis=0)

time: 56.7 us -> 52.2 us (0.921)
  blocking collectives: 35.4 us -> 30.9 us
    psum x1 -> x0, blocking collectives: 15.2 us -> none  [on_device(): gains = lax.psum(partial_value, 'pts')]
    all_gather x0 -> x1, blocking collectives: none -> 10.6 us  [on_device(): y1 = lax.all_gather(partial_value, 'pts')]
where the time goes in v1:
time: 52.2 us; the launch traced here: 52 us
  blocking collectives  30.9 us (59%)
  other arithmetic  13.9 us (27%)
  matrix products  4.37 us (8%)
  local copies, waits for them, and re-layouts  1.5 us (3%)
  between operations  1.35 us (3%)
    unnamed x1, blocking collectives  11.9 us
    all_gather x1, blocking collectives, on_device(): y1 = lax.all_gather(partial_value, 'pts')  10.6 us
    pmax x1, blocking collectives, on_device(): best_sim = lax.pmax(local_best, 'cand')  8.34 us
    top_k x3, other arithmetic, best_values(): return lax.top_k(jnp.concatenate([first, second]), TOPK)[0]  7.7 us
    top_k x1, other arithmetic, on_device(): top_gains = joined(lax.top_k(gains, TOPK)[0], 'cand', best_values)  4.43 us
    dot_general x1, matrix products, on_device(): jnp.dot(points, candidates.T, preferred_element_type=jnp.float32) * scale  4.37 us
    unnamed x13, local copies, waits for them, and re-layouts  1.38 us

profile of v1, /device:TPU:0, one launch (start us, length us, event | category | flops | bytes accessed | tf_op | source)
XLA Modules:
  0.0 52.0 jit_solution(10120818668522465942)
XLA Ops:
  0.6 0.0 copy-start
  0.7 0.9 %compare_reduce_fusion = pred[1024]{0:T(1024)(128)(4,1)S(1)} fusion(s32[1024]{0:T(1024)S(1)} %iota_add_fusion, s32[64]{0:T(128)} %param.11), kind=kLoop, calls=%fused_computation.4 | loop fusion | flops 130048 | bytes 5376 | tf_op jit(solution)/shard_map/reduce_or | solution.py:36
  1.6 0.7 %copy-done = bf16[1024,1024]{1,0:T(8,128)(2,1)S(1)} copy-done((bf16[1024,1024]{1,0:T(8,128)(2,1)S(1)}, bf16[1024,1024]{1,0:T(8,128)(2,1)}, u32[]{:S(2)}) %copy-start) | copy-done | bytes 2097176
  2.2 0.0 copy-start.3
  2.2 0.0 copy-start.2
  2.2 4.4 %select_reduce_fusion = (f32[1024]{0:T(1024)S(1)}, f32[1024]{0:T(1024)S(1)}) fusion(pred[1024]{0:T(1024)(128)(4,1)S(1)} %compare_reduce_fusion, f32[1024]{0:T(1024)} %param.9, f32[1024]{0:T(1024)} %param.8, bf16[1024,1024]{1,0:T(8,128)(2,1)S(1)} %copy-done, bf16[1024,1024]{1,0:T(8,128)(2,1)} %param.10), kind=kOutput, calls=%fused_computation.2 | convolution fusion | flops 2154821632 | bytes 4211712 | tf_op jit(solution)/shard_map/dot_general | solution.py:28
  6.6 10.6 %all-gather = f32[8192]{0:T(1024)S(1)} all-gather(f32[1024]{0:T(1024)S(1)} %broadcast_multiply_fusion), channel_id=2, replica_groups=mesh['pts'=8,'cand'=4] {'pts'}, dimensions={0}, use_global_device_ids=true | all-gather | bytes 36864 | tf_op jit(solution)/shard_map/all_gather | solution.py:32
  17.3 0.0 copy-start.1
  17.3 4.4 %top_k.14 = (f32[1024]{0:T(1024)S(1)}, s32[1024]{0:T(1024)}) sort(f32[1024]{0:T(1024)S(1)} %reduce_sum.19, s32[1024]{0:T(1024)S(1)} %iota.11), dimensions={0}, to_apply=%region_2.0 | sort | flops 10240 | bytes 16384 | tf_op jit(solution)/shard_map/top_k | solution.py:34
  21.7 0.0 copy-done.3
  21.7 0.6 %dynamic-slice = u32[1]{0:T(128)} dynamic-slice(u32[32]{0:T(128)S(1)} %copy-done.3, u32[]{:T(128)S(6)} %add.45), dynamic_slice_sizes={1} | dynamic-slice | bytes 12
  23.0 0.1 slice_dynamic-update-slice_fusion
  23.1 11.9 %all-reduce = f32[256]{0:T(256)S(1)} all-reduce(f32[256]{0:T(256)S(1)} %slice_dynamic-update-slice_fusion), channel_id=3, replica_groups=mesh['pts'=8,'cand'=4] {'cand'}, use_global_device_ids=true, to_apply=%add | all-reduce | flops 256 | bytes 2048
  35.0 0.1 reshape.24
  35.1 8.0 %while.15 = (s32[]{:T(128)}, f32[64]{0:T(128)S(1)}, f32[4,64]{1,0:T(4,128)S(1)}, s32[]{:T(128)}, s32[]{:T(128)}, /*index=5*/s32[]{:T(128)}) while((s32[]{:T(128)}, f32[64]{0:T(128)S(1)}, f32[4,64]{1,0:T(4,128)S(1)}, s32[]{:T(128)}, s32[]{:T(128)}, /*index=5*/s32[]{:T(128)}) %tuple.41), condition=%wide.region_5.6_spmd, body=%wide.region_3.5_spmd.sunk | while | flops 1029 | bytes 4211 | solution.py:16
  35.1 0.1 pad_maximum_fusion.2
  35.2 2.6 %top_k.22 = (f32[128]{0:T(128)S(1)}, s32[128]{0:T(128)}) sort(f32[128]{0:T(128)S(1)} %pad_maximum_fusion.2, s32[128]{0:T(128)S(1)} %iota.15), dimensions={0}, to_apply=%region_4.4 | sort | flops 896 | bytes 2048 | tf_op jit(solution)/shard_map/while/body/eval_jaxpr/top_k | solution.py:20
  37.7 0.1 pad_maximum_fusion.2
  37.8 2.6 %top_k.22 = (f32[128]{0:T(128)S(1)}, s32[128]{0:T(128)}) sort(f32[128]{0:T(128)S(1)} %pad_maximum_fusion.2, s32[128]{0:T(128)S(1)} %iota.15), dimensions={0}, to_apply=%region_4.4 | sort | flops 896 | bytes 2048 | tf_op jit(solution)/shard_map/while/body/eval_jaxpr/top_k | solution.py:20
  40.4 0.1 pad_maximum_fusion.2
  40.5 2.6 %top_k.22 = (f32[128]{0:T(128)S(1)}, s32[128]{0:T(128)}) sort(f32[128]{0:T(128)S(1)} %pad_maximum_fusion.2, s32[128]{0:T(128)S(1)} %iota.15), dimensions={0}, to_apply=%region_4.4 | sort | flops 896 | bytes 2048 | tf_op jit(solution)/shard_map/while/body/eval_jaxpr/top_k | solution.py:20
  43.0 0.0 copy-start.4
  43.0 8.3 %pmax.7 = f32[1024]{0:T(1024)S(1)} all-reduce(f32[1024]{0:T(1024)S(1)} %get-tuple-element.97), channel_id=1, replica_groups=mesh['pts'=8,'cand'=4] {'cand'}, use_global_device_ids=true, to_apply=%region_8.9 | all-reduce | flops 1024 | bytes 8192 | tf_op jit(solution)/shard_map/pmax | solution.py:38
  51.4 0.0 copy-done.2
  51.4 0.6 %max.13 = f32[1024]{0:T(1024)} maximum(f32[1024]{0:T(1024)S(1)} %copy-done.2, f32[1024]{0:T(1024)S(1)} %pmax.7) | non-fusion elementwise | flops 1024 | bytes 12288 | tf_op jit(solution)/shard_map/max | solution.py:39
  52.0 0.0 copy-done.1
  52.0 0.0 copy-done.4
  (13 shorter events, 0.1 us)
Async XLA Ops:
  0.6 1.6 %copy-start = (bf16[1024,1024]{1,0:T(8,128)(2,1)S(1)}, bf16[1024,1024]{1,0:T(8,128)(2,1)}, u32[]{:S(2)}) copy-start(bf16[1024,1024]{1,0:T(8,128)(2,1)} %param.7) | copy-start | bytes 6291460
  2.2 19.5 %copy-start.3 = (u32[32]{0:T(128)S(1)}, u32[32]{0:T(128)}, u32[]{:S(2)}) copy-start(u32[32]{0:T(128)} %constant.74) | copy-start | bytes 388
  2.2 49.1 %copy-start.2 = (f32[1024]{0:T(1024)S(1)}, f32[1024]{0:T(1024)}, u32[]{:S(2)}) copy-start(f32[1024]{0:T(1024)} %param.9) | copy-start | bytes 12292
  17.3 34.7 %copy-start.1 = (f32[1024]{0:T(1024)}, f32[1024]{0:T(1024)S(1)}, u32[]{:S(2)}) copy-start(f32[1024]{0:T(1024)S(1)} %reduce_sum.19) | copy-start | bytes 12292
  43.0 8.9 %copy-start.4 = (f32[64]{0:T(128)}, f32[64]{0:T(128)S(1)}, u32[]{:S(2)}) copy-start(f32[64]{0:T(128)S(1)} %get-tuple-element.93) | copy-start | bytes 772
